TPU v7x, 32 devices: a whole 2x2x4 slice. The times are simulated.
32 devices in a mesh: row: 4 (over z), col: 8 (over y, x, core).
Axes of the slice: x: 2, y: 2, z: 4, core: 2. Of those that a mesh axis runs over, the one named last changes fastest.
Arguments:
- front: float32 [12288, 12288], P('row', 'col'), as said below
- structure: int32 [3, 96], replicated, may hold values from 0 to 1, as said below
- factor_front: float32 [3, 12288, 512], P(None, 'row', 'col'), may hold values from -0.0546875 to 0.0546875
- factor_border: float32 [2, 512, 512], replicated, may hold values from -0.6 to 0.6
- pivot_inverse: float32 [3, 512, 512], P(None, 'row')
Outputs:
- inverse_front: float32 [3, 512, 12288], P(None, 'row', 'col')
- inverse_parent: float32 [2, 512, 512], P(None, 'row')
- inverse_diagonal: float32 [3, 512, 512], P(None, 'row')
Inputs may be any that keep to these rules, and one draw needn't show every extreme that they name: front is exactly symmetric. structure[k, b] = 1 where front block b (rows b * 128 to (b + 1) * 128 - 1) lies in supernode k's structure; every 1 in row k is also a 1 in row k - 1; blocks b < 24 are 1 in every row.
All inputs are finite; a program needn't handle non-finite values.
Results may differ from a plain program's by a relative error of at most 0.0001.
Values sent between devices are 32-bit elements; how exact they have to be, the bound alone decides.
No kernel may reach another device: no remote copies, remote signals or barrier semaphores. Data moves between devices by JAX's collectives and lax.ppermute only.
A program may use at most 128 MiB of HBM per device.

v0:
```python
import jax
import jax.numpy as jnp
from jax import lax
from jax.sharding import PartitionSpec as P

BLK = 128
HIGH = lax.Precision.HIGHEST


def broadcast(x, axis, root):
    mine = lax.axis_index(axis) == root
    return lax.psum(jnp.where(mine, x, jnp.zeros_like(x)), axis)


def matmul(former, latter):
    return jnp.dot(former, latter, precision=HIGH, preferred_element_type=jnp.float32)


def contract_first(former, latter):
    return lax.dot_general(
        former, latter, (((0,), (0,)), ((), ())), precision=HIGH, preferred_element_type=jnp.float32
    )


def block_flags(structure_row, first_row, rows_count):
    position = first_row + jnp.arange(rows_count, dtype=jnp.int32)
    owners = position // BLK
    numbers = jnp.arange(structure_row.shape[0], dtype=jnp.int32)
    matches = (owners[:, None] == numbers[None, :]).astype(jnp.float32)
    return jnp.dot(matches, structure_row.astype(jnp.float32), precision=HIGH)


def body(front, structure, factor_front, factor_border, pivot_inverse):
    row_index = lax.axis_index("row")
    col_index = lax.axis_index("col")
    rows_here = front.shape[0]
    cols_here = front.shape[1]
    width_here = pivot_inverse.shape[1]
    supers = structure.shape[0]
    row_first = row_index * rows_here
    col_first = col_index * cols_here
    fronts = []
    parents = []
    diagonals = []
    previous = None
    diag_prev = None
    for section in range(supers):
        gathered = lax.all_gather(factor_front[section], "col", axis=1, tiled=True)
        row_flags = block_flags(structure[section], row_first, rows_here)
        factor_rows = gathered * row_flags[:, None]
        own_half = lax.dynamic_slice_in_dim(factor_rows, col_index % 2 * cols_here, cols_here, 0)
        factor_cols = broadcast(own_half, "row", col_index // 2)
        partial_value = contract_first(factor_rows, front)
        if section > 0:
            border = factor_border[section - 1]
            border_rows = lax.dynamic_slice_in_dim(border, row_index * width_here, width_here, 0)
            partial_value = partial_value + contract_first(border_rows, previous)
            parent_part = lax.psum(matmul(previous, factor_cols), "col")
            parent_rows = parent_part + matmul(diag_prev, border)
            parent_all = lax.all_gather(parent_rows, "row", axis=0, tiled=True)
            parents.append(-parent_rows)
        image_rows = lax.psum_scatter(partial_value, "row", scatter_dimension=0, tiled=True)
        col_flags = block_flags(structure[section], col_first, cols_here)
        current = -(image_rows * col_flags[None, :])
        gram_rows = lax.psum(matmul(image_rows, factor_cols), "col")
        diag_now = pivot_inverse[section] + gram_rows
        if section > 0:
            parent_slice = lax.dynamic_slice_in_dim(
                parent_all, row_index * width_here, width_here, 1
            )
            diag_now = diag_now + contract_first(parent_slice, border)
        fronts.append(current)
        diagonals.append(diag_now)
        previous = current
        diag_prev = diag_now
    return (jnp.stack(fronts), jnp.stack(parents), jnp.stack(diagonals))


def solution(mesh):
    placed = (P("row", "col"), P(), P(None, "row", "col"), P(), P(None, "row", None))
    return jax.shard_map(
        body,
        mesh=mesh,
        in_specs=placed,
        out_specs=(P(None, "row", "col"), P(None, "row", None), P(None, "row", None)),
        check_vma=False,
    )
```

profile of v0, /device:TPU:0, one launch (start us, length us, event | category | flops | bytes accessed | tf_op | source)
XLA Modules:
  0.0 802.7 jit_solution(8092300581253794925)
XLA Ops:
  7.2 3.1 fusion.61
  13.2 45.4 %all-gather.13.cloned.1.call-done = f32[1,3072,512]{1,2,0:T(8,128)} async-done(((f32[1,3072,64]{1,2,0:T(8,128)}), f32[1,3072,512]{1,2,0:T(8,128)}) %all-gather.13.cloned.1.call-update) | async-done | bytes 6291472 | tf_op jit(solution)/shard_map/all_gather | solution.py:48
  58.6 3.4 bitcast_multiply_fusion.2
  62.0 2.6 copy-done.1
  64.7 33.4 %fusion.63 = f32[512,1536]{1,0:T(8,128)} fusion(f32[3072,512]{0,1:T(8,128)S(1)} %bitcast_multiply_fusion.2, f32[3072,1536]{1,0:T(8,128)} %param.5), kind=kOutput, calls=%fused_computation.103 | convolution fusion | flops 28991029248 | bytes 28311552 | tf_op jit(solution)/shard_map/dot_general | solution.py:20
  103.0 2.9 all-gather.15.cloned.1.call-done
  105.9 3.4 bitcast_multiply_fusion.1
  109.3 2.6 copy-done.2
  111.9 33.4 %fusion.64 = f32[512,1536]{1,0:T(8,128)} fusion(f32[3072,512]{0,1:T(8,128)S(1)} %bitcast_multiply_fusion.1, f32[3072,1536]{1,0:T(8,128)} %param.5), kind=kOutput, calls=%fused_computation.104 | convolution fusion | flops 28991029248 | bytes 28311552 | tf_op jit(solution)/shard_map/dot_general | solution.py:20
  145.3 23.4 %reduce-scatter.4.cloned.1.call-done = f32[128,1536]{1,0:T(8,128)} async-done(((f32[512,1536]{1,0:T(8,128)}), f32[128,1536]{1,0:T(8,128)}) %reduce-scatter.4.cloned.1.call-update) | async-done | bytes 786448 | tf_op jit(solution)/shard_map/reduce_scatter | solution.py:62
  168.6 6.6 convolution_add_fusion.1
  177.5 4.1 dynamic-slice_select_fusion.2
  181.6 3.8 dynamic-slice_select_fusion.1
  185.4 30.3 %all-gather.17.cloned.1.call-done = f32[1,3072,512]{1,2,0:T(8,128)} async-done(((f32[1,3072,64]{1,2,0:T(8,128)}), f32[1,3072,512]{1,2,0:T(8,128)}) %all-gather.17.cloned.1.call-update) | async-done | bytes 6291472 | tf_op jit(solution)/shard_map/all_gather | solution.py:48
  215.7 3.4 bitcast_multiply_fusion
  219.1 2.6 copy-done.3
  224.4 35.4 %fusion.65 = f32[512,1536]{1,0:T(8,128)} fusion(f32[3072,512]{0,1:T(8,128)} %copy-done.3, f32[3072,1536]{1,0:T(8,128)} %param.5), kind=kOutput, calls=%fused_computation.105 | convolution fusion | flops 28991029248 | bytes 28311552 | tf_op jit(solution)/shard_map/dot_general | solution.py:20
  259.8 18.5 %reduce-scatter.6.cloned.1.call-done = f32[128,1536]{1,0:T(8,128)} async-done(((f32[512,1536]{1,0:T(8,128)}), f32[128,1536]{1,0:T(8,128)}) %reduce-scatter.6.cloned.1.call-update) | async-done | bytes 786448 | tf_op jit(solution)/shard_map/reduce_scatter | solution.py:62
  278.3 5.6 convolution_add_fusion
  284.2 321.4 %all-reduce.7.cloned.1.call-done = (f32[1536,512]{0,1:T(8,128)}, f32[1536,512]{0,1:T(8,128)}, f32[1536,512]{0,1:T(8,128)}) async-done(((f32[1536,512]{0,1:T(8,128)}, f32[1536,512]{0,1:T(8,128)}, f32[1536,512]{0,1:T(8,128)}), (f32[1536,512]{0,1:T(8,128)}, f32[1536,512]{0,1:T(8,128)}, f32[1536,512]{0,1:T(8,128)})) %all-reduce.7.cloned.1.call-update) | async-done | bytes 9437200 | tf_op jit(solution)/shard_map/psum | solution.py:12
  605.6 6.0 fusion.66
  611.6 3.9 fusion.11
  615.5 4.0 fusion.67
  619.6 3.9 fusion.13
  623.4 43.9 %reduce-scatter.8.cloned.1.call-done = f32[128,1536]{1,0:T(8,128)} async-done(((f32[512,1536]{1,0:T(8,128)}), f32[128,1536]{1,0:T(8,128)}) %reduce-scatter.8.cloned.1.call-update) | async-done | bytes 786448 | tf_op jit(solution)/shard_map/reduce_scatter | solution.py:62
  667.3 6.1 fusion.68
  673.8 58.5 %all-reduce.5.cloned.1.call-done = (f32[128,512]{1,0:T(8,128)}, f32[128,512]{1,0:T(8,128)}, f32[128,512]{1,0:T(8,128)}, f32[128,512]{1,0:T(8,128)}, f32[128,512]{1,0:T(8,128)}) async-done(((f32[128,512]{1,0:T(8,128)}, f32[128,512]{1,0:T(8,128)}, f32[128,512]{1,0:T(8,128)}, f32[128,512]{1,0:T(8,128)}, f32[128,512]{1,0:T(8,128)}), (f32[128,512]{1,0:T(8,128)}, f32[128,512]{1,0:T(8,128)}, f32[128,512]{1,0:T(8,128)}, ...) | async-done | bytes 1310736 | tf_op jit(solution)/shard_map/psum | solution.py:58
  732.3 2.5 convolution_add_fusion.5
  736.5 2.2 fusion.14
  738.7 23.4 %all-gather.9.cloned.1.call-done = f32[512,512]{1,0:T(8,128)} async-done(((f32[128,512]{1,0:T(8,128)}), f32[512,512]{1,0:T(8,128)}) %all-gather.9.cloned.1.call-update) | async-done | bytes 1048592 | tf_op jit(solution)/shard_map/all_gather | solution.py:60
  765.5 3.0 pad_maximum_fusion
  770.4 22.5 %all-gather.11.cloned.1.call-done = f32[512,512]{1,0:T(8,128)} async-done(((f32[128,512]{1,0:T(8,128)}), f32[512,512]{1,0:T(8,128)}) %all-gather.11.cloned.1.call-update) | async-done | bytes 1048592 | tf_op jit(solution)/shard_map/all_gather | solution.py:60
  (67 shorter events, 22.8 us)
Async XLA Ops:
  7.2 4.0 copy-start.14
  7.2 51.4 %all-gather.13.cloned.1.call-start = ((), (), s32[]{:S(2)}) async-start(), calls=%async_computation.8 | async-start | bytes 7077888 | tf_op jit(solution)/shard_map/all_gather | solution.py:48
  10.3 95.6 %all-gather.15.cloned.1.call-start = ((), (), s32[]{:S(2)}) async-start(), calls=%async_computation.9 | async-start | bytes 7077888 | tf_op jit(solution)/shard_map/all_gather | solution.py:48
  11.1 157.6 %reduce-scatter.4.cloned.1.call-start = ((), (), s32[]{:S(2)}) async-start(), calls=%async_computation.3 | async-start | bytes 3932160 | tf_op jit(solution)/shard_map/reduce_scatter | solution.py:62
  62.0 2.7 copy-start.1
  98.0 3.8 copy-start
  98.1 117.6 %all-gather.17.cloned.1.call-start = ((), (), s32[]{:S(2)}) async-start(), calls=%async_computation.10 | async-start | bytes 7077888 | tf_op jit(solution)/shard_map/all_gather | solution.py:48
  98.6 179.6 %reduce-scatter.6.cloned.1.call-start = ((), (), s32[]{:S(2)}) async-start(), calls=%async_computation.4 | async-start | bytes 3932160 | tf_op jit(solution)/shard_map/reduce_scatter | solution.py:62
  109.3 2.6 copy-start.2
  175.3 430.3 %all-reduce.7.cloned.1.call-start = ((), (), s32[]{:S(2)}) async-start(), calls=%async_computation.12 | async-start | bytes 18874368 | tf_op jit(solution)/shard_map/psum | solution.py:12
  219.1 2.7 copy-start.3
  223.7 443.5 %reduce-scatter.8.cloned.1.call-start = ((), (), s32[]{:S(2)}) async-start(), calls=%async_computation.5 | async-start | bytes 3932160 | tf_op jit(solution)/shard_map/reduce_scatter | solution.py:62
  283.9 321.7 %copy-start.4 = (f32[128,1536]{1,0:T(8,128)S(1)}, f32[128,1536]{1,0:T(8,128)}, u32[]{:S(2)}) copy-start(f32[128,1536]{1,0:T(8,128)} %reduce-scatter.4.cloned.1.call-done) | copy-start | bytes 2359300
  284.0 448.3 %all-reduce.5.cloned.1.call-start = ((), (), s32[]{:S(2)}) async-start(), calls=%async_computation.11 | async-start | bytes 2621440 | tf_op jit(solution)/shard_map/psum | solution.py:58
  605.6 6.0 copy-start.7
  611.6 3.9 copy-start.5
  615.5 4.0 copy-start.6
  673.5 88.6 %all-gather.9.cloned.1.call-start = ((), (), s32[]{:S(2)}) async-start(), calls=%async_computation.6 | async-start | bytes 1310720 | tf_op jit(solution)/shard_map/all_gather | solution.py:60
  734.8 29.1 %copy-start.13 = (f32[128,512]{1,0:T(8,128)S(1)}, f32[128,512]{1,0:T(8,128)}, u32[]{:S(2)}) copy-start(f32[128,512]{1,0:T(8,128)} %get-tuple-element.3) | copy-start | bytes 786436
  734.8 58.1 %all-gather.11.cloned.1.call-start = ((), (), s32[]{:S(2)}) async-start(), calls=%async_computation.7 | async-start | bytes 1310720 | tf_op jit(solution)/shard_map/all_gather | solution.py:60
  736.5 28.9 %copy-start.8 = (f32[128,1536]{1,0:T(8,128)S(1)}, f32[128,1536]{1,0:T(8,128)}, u32[]{:S(2)}) copy-start(f32[128,1536]{1,0:T(8,128)} %reduce-scatter.8.cloned.1.call-done) | copy-start | bytes 2359300
  765.4 3.1 copy-start.10
  765.4 3.1 copy-start.11
  765.5 4.0 copy-start.9
  765.5 27.4 %copy-start.12 = (f32[128,512]{1,0:T(8,128)S(1)}, f32[128,512]{1,0:T(8,128)}, u32[]{:S(2)}) copy-start(f32[128,512]{1,0:T(8,128)} %get-tuple-element.7) | copy-start | bytes 786436
Sparse Core Ops, SparseCore 0:
  10.5 48.1 all-gather.12
  60.5 45.3 all-gather.14
  108.2 60.3 reduce-scatter.3
  170.4 45.2 all-gather.16
  217.9 60.3 reduce-scatter.5
  281.0 324.5 all-reduce.6
  607.9 59.3 reduce-scatter.7
  673.6 58.6 all-reduce.4
  735.0 27.0 all-gather.8
  765.5 27.3 all-gather.10
where the time goes:
time: 809 us; the launch traced here: 803 us
  waiting for transfers between devices  591 us (73%)
  matrix products  154 us (19%)
  other arithmetic  29 us (4%)
  between operations  14.7 us (2%)
  local copies, waits for them, and re-layouts  12.1 us (1%)
    psum x1, waiting for transfers between devices, broadcast(): return lax.psum(jnp.where(mine, x, jnp.zeros_like(x)), axis)  321 us
    dot_general x7, matrix products, contract_first(): lax.dot_general(former, latter, (((0,), (0,)), ((), ())), precision=HIGH,...  118 us
    reduce_scatter x3, waiting for transfers between devices, body(): lax.psum_scatter(partial_value, 'row', scatter_dimension=0, tiled=True)  85.7 us
    all_gather x3, waiting for transfers between devices, body(): gathered = lax.all_gather(factor_front[section], 'col', axis=1, tiled=True)  78.7 us
    psum x1, waiting for transfers between devices, body(): parent_part = lax.psum(matmul(previous, factor_cols), 'col')  58.5 us
    all_gather x2, waiting for transfers between devices, body(): parent_all = lax.all_gather(parent_rows, 'row', axis=0, tiled=True)  45.9 us
    dot_general x7, matrix products, matmul(): jnp.dot(former, latter, precision=HIGH, preferred_element_type=jnp.float32)  27.9 us
  transfers between devices with their start and end apart: 10, of which 10 were waited for; matrix products, arithmetic and copies ran while one was open for 21% of the time, Pallas kernels for 0%

commit v1 on v0

--- a/solution.py
+++ b/solution.py
@@ -45,7 +45,7 @@
     previous = None
     diag_prev = None
     for section in range(supers):
-        gathered = lax.all_gather(factor_front[section], "col", axis=1, tiled=True)
+        gathered = jnp.concatenate(lax.all_gather(factor_front[section], "col"), axis=1)
         row_flags = block_flags(structure[section], row_first, rows_here)
         factor_rows = gathered * row_flags[:, None]
         own_half = lax.dynamic_slice_in_dim(factor_rows, col_index % 2 * cols_here, cols_here, 0)

time: 809 us -> 809 us (level)
  no operation moved by 1% of the time
where the time goes in v1:
time: 809 us; the launch traced here: 803 us
  waiting for transfers between devices  591 us (73%)
  matrix products  154 us (19%)
  other arithmetic  29 us (4%)
  between operations  14.7 us (2%)
  local copies, waits for them, and re-layouts  12.1 us (1%)
    psum x1, waiting for transfers between devices, broadcast(): return lax.psum(jnp.where(mine, x, jnp.zeros_like(x)), axis)  321 us
    dot_general x7, matrix products, contract_first(): lax.dot_general(former, latter, (((0,), (0,)), ((), ())), precision=HIGH,...  118 us
    reduce_scatter x3, waiting for transfers between devices, body(): lax.psum_scatter(partial_value, 'row', scatter_dimension=0, tiled=True)  85.7 us
    all_gather x3, waiting for transfers between devices, body(): lax.all_gather(factor_front[section], 'col')  78.7 us
    psum x1, waiting for transfers between devices, body(): parent_part = lax.psum(matmul(previous, factor_cols), 'col')  58.5 us
    all_gather x2, waiting for transfers between devices, body(): parent_all = lax.all_gather(parent_rows, 'row', axis=0, tiled=True)  45.9 us
    dot_general x7, matrix products, matmul(): jnp.dot(former, latter, precision=HIGH, preferred_element_type=jnp.float32)  27.9 us
  transfers between devices with their start and end apart: 10, of which 10 were waited for; matrix products, arithmetic and copies ran while one was open for 21% of the time, Pallas kernels for 0%

profile of v1, /device:TPU:0, one launch (start us, length us, event | category | flops | bytes accessed | tf_op | source)
XLA Modules:
  0.0 802.7 jit_solution(8092300581253794925)
XLA Ops:
  7.2 3.1 fusion.61
  13.2 45.4 %all-gather.6.cloned.1.call-done = f32[8,3072,64]{1,2,0:T(8,128)} async-done(((f32[1,3072,64]{1,2,0:T(8,128)}), f32[8,3072,64]{1,2,0:T(8,128)}) %all-gather.6.cloned.1.call-update) | async-done | bytes 6291472 | tf_op jit(solution)/shard_map/all_gather | solution.py:48
  58.6 3.4 bitcast_multiply_fusion.2
  62.0 2.6 copy-done.1
  64.7 33.4 %fusion.63 = f32[512,1536]{1,0:T(8,128)} fusion(f32[3072,512]{0,1:T(8,128)S(1)} %bitcast_multiply_fusion.2, f32[3072,1536]{1,0:T(8,128)} %param.5), kind=kOutput, calls=%fused_computation.103 | convolution fusion | flops 28991029248 | bytes 28311552 | tf_op jit(solution)/shard_map/dot_general | solution.py:20
  103.0 2.9 all-gather.8.cloned.1.call-done
  105.9 3.4 bitcast_multiply_fusion.1
  109.3 2.6 copy-done.2
  111.9 33.4 %fusion.64 = f32[512,1536]{1,0:T(8,128)} fusion(f32[3072,512]{0,1:T(8,128)S(1)} %bitcast_multiply_fusion.1, f32[3072,1536]{1,0:T(8,128)} %param.5), kind=kOutput, calls=%fused_computation.104 | convolution fusion | flops 28991029248 | bytes 28311552 | tf_op jit(solution)/shard_map/dot_general | solution.py:20
  145.3 23.4 %reduce-scatter.4.cloned.1.call-done = f32[128,1536]{1,0:T(8,128)} async-done(((f32[512,1536]{1,0:T(8,128)}), f32[128,1536]{1,0:T(8,128)}) %reduce-scatter.4.cloned.1.call-update) | async-done | bytes 786448 | tf_op jit(solution)/shard_map/reduce_scatter | solution.py:62
  168.6 6.6 convolution_add_fusion.1
  177.5 4.1 dynamic-slice_select_fusion.2
  181.6 3.8 dynamic-slice_select_fusion.1
  185.4 30.3 %all-gather.10.cloned.1.call-done = f32[8,3072,64]{1,2,0:T(8,128)} async-done(((f32[1,3072,64]{1,2,0:T(8,128)}), f32[8,3072,64]{1,2,0:T(8,128)}) %all-gather.10.cloned.1.call-update) | async-done | bytes 6291472 | tf_op jit(solution)/shard_map/all_gather | solution.py:48
  215.7 3.4 bitcast_multiply_fusion
  219.1 2.6 copy-done.3
  224.4 35.4 %fusion.65 = f32[512,1536]{1,0:T(8,128)} fusion(f32[3072,512]{0,1:T(8,128)} %copy-done.3, f32[3072,1536]{1,0:T(8,128)} %param.5), kind=kOutput, calls=%fused_computation.105 | convolution fusion | flops 28991029248 | bytes 28311552 | tf_op jit(solution)/shard_map/dot_general | solution.py:20
  259.8 18.5 %reduce-scatter.6.cloned.1.call-done = f32[128,1536]{1,0:T(8,128)} async-done(((f32[512,1536]{1,0:T(8,128)}), f32[128,1536]{1,0:T(8,128)}) %reduce-scatter.6.cloned.1.call-update) | async-done | bytes 786448 | tf_op jit(solution)/shard_map/reduce_scatter | solution.py:62
  278.3 5.6 convolution_add_fusion
  284.2 321.4 %all-reduce.7.cloned.1.call-done = (f32[1536,512]{0,1:T(8,128)}, f32[1536,512]{0,1:T(8,128)}, f32[1536,512]{0,1:T(8,128)}) async-done(((f32[1536,512]{0,1:T(8,128)}, f32[1536,512]{0,1:T(8,128)}, f32[1536,512]{0,1:T(8,128)}), (f32[1536,512]{0,1:T(8,128)}, f32[1536,512]{0,1:T(8,128)}, f32[1536,512]{0,1:T(8,128)})) %all-reduce.7.cloned.1.call-update) | async-done | bytes 9437200 | tf_op jit(solution)/shard_map/psum | solution.py:12
  605.6 6.0 fusion.66
  611.6 3.9 fusion.11
  615.5 4.0 fusion.67
  619.6 3.9 fusion.13
  623.4 43.9 %reduce-scatter.8.cloned.1.call-done = f32[128,1536]{1,0:T(8,128)} async-done(((f32[512,1536]{1,0:T(8,128)}), f32[128,1536]{1,0:T(8,128)}) %reduce-scatter.8.cloned.1.call-update) | async-done | bytes 786448 | tf_op jit(solution)/shard_map/reduce_scatter | solution.py:62
  667.3 6.1 fusion.68
  673.8 58.5 %all-reduce.5.cloned.1.call-done = (f32[128,512]{1,0:T(8,128)}, f32[128,512]{1,0:T(8,128)}, f32[128,512]{1,0:T(8,128)}, f32[128,512]{1,0:T(8,128)}, f32[128,512]{1,0:T(8,128)}) async-done(((f32[128,512]{1,0:T(8,128)}, f32[128,512]{1,0:T(8,128)}, f32[128,512]{1,0:T(8,128)}, f32[128,512]{1,0:T(8,128)}, f32[128,512]{1,0:T(8,128)}), (f32[128,512]{1,0:T(8,128)}, f32[128,512]{1,0:T(8,128)}, f32[128,512]{1,0:T(8,128)}, ...) | async-done | bytes 1310736 | tf_op jit(solution)/shard_map/psum | solution.py:58
  732.3 2.5 convolution_add_fusion.5
  736.5 2.2 fusion.14
  738.7 23.4 %all-gather.12.cloned.1.call-done = f32[512,512]{1,0:T(8,128)} async-done(((f32[128,512]{1,0:T(8,128)}), f32[512,512]{1,0:T(8,128)}) %all-gather.12.cloned.1.call-update) | async-done | bytes 1048592 | tf_op jit(solution)/shard_map/all_gather | solution.py:60
  765.5 3.0 pad_maximum_fusion
  770.4 22.5 %all-gather.14.cloned.1.call-done = f32[512,512]{1,0:T(8,128)} async-done(((f32[128,512]{1,0:T(8,128)}), f32[512,512]{1,0:T(8,128)}) %all-gather.14.cloned.1.call-update) | async-done | bytes 1048592 | tf_op jit(solution)/shard_map/all_gather | solution.py:60
  (67 shorter events, 22.8 us)
Async XLA Ops:
  7.2 4.0 copy-start.14
  7.2 51.4 %all-gather.6.cloned.1.call-start = ((), (), s32[]{:S(2)}) async-start(), calls=%async_computation.3 | async-start | bytes 7077888 | tf_op jit(solution)/shard_map/all_gather | solution.py:48
  10.3 95.6 %all-gather.8.cloned.1.call-start = ((), (), s32[]{:S(2)}) async-start(), calls=%async_computation.5 | async-start | bytes 7077888 | tf_op jit(solution)/shard_map/all_gather | solution.py:48
  11.1 157.6 %reduce-scatter.4.cloned.1.call-start = ((), (), s32[]{:S(2)}) async-start(), calls=%async_computation.4 | async-start | bytes 3932160 | tf_op jit(solution)/shard_map/reduce_scatter | solution.py:62
  62.0 2.7 copy-start.1
  98.0 3.8 copy-start
  98.1 117.6 %all-gather.10.cloned.1.call-start = ((), (), s32[]{:S(2)}) async-start(), calls=%async_computation.7 | async-start | bytes 7077888 | tf_op jit(solution)/shard_map/all_gather | solution.py:48
  98.6 179.6 %reduce-scatter.6.cloned.1.call-start = ((), (), s32[]{:S(2)}) async-start(), calls=%async_computation.6 | async-start | bytes 3932160 | tf_op jit(solution)/shard_map/reduce_scatter | solution.py:62
  109.3 2.6 copy-start.2
  175.3 430.3 %all-reduce.7.cloned.1.call-start = ((), (), s32[]{:S(2)}) async-start(), calls=%async_computation.12 | async-start | bytes 18874368 | tf_op jit(solution)/shard_map/psum | solution.py:12
  219.1 2.7 copy-start.3
  223.7 443.5 %reduce-scatter.8.cloned.1.call-start = ((), (), s32[]{:S(2)}) async-start(), calls=%async_computation.8 | async-start | bytes 3932160 | tf_op jit(solution)/shard_map/reduce_scatter | solution.py:62
  283.9 321.7 %copy-start.4 = (f32[128,1536]{1,0:T(8,128)S(1)}, f32[128,1536]{1,0:T(8,128)}, u32[]{:S(2)}) copy-start(f32[128,1536]{1,0:T(8,128)} %reduce-scatter.4.cloned.1.call-done) | copy-start | bytes 2359300
  284.0 448.3 %all-reduce.5.cloned.1.call-start = ((), (), s32[]{:S(2)}) async-start(), calls=%async_computation.11 | async-start | bytes 2621440 | tf_op jit(solution)/shard_map/psum | solution.py:58
  605.6 6.0 copy-start.7
  611.6 3.9 copy-start.5
  615.5 4.0 copy-start.6
  673.5 88.6 %all-gather.12.cloned.1.call-start = ((), (), s32[]{:S(2)}) async-start(), calls=%async_computation.9 | async-start | bytes 1310720 | tf_op jit(solution)/shard_map/all_gather | solution.py:60
  734.8 29.1 %copy-start.13 = (f32[128,512]{1,0:T(8,128)S(1)}, f32[128,512]{1,0:T(8,128)}, u32[]{:S(2)}) copy-start(f32[128,512]{1,0:T(8,128)} %get-tuple-element.3) | copy-start | bytes 786436
  734.8 58.1 %all-gather.14.cloned.1.call-start = ((), (), s32[]{:S(2)}) async-start(), calls=%async_computation.10 | async-start | bytes 1310720 | tf_op jit(solution)/shard_map/all_gather | solution.py:60
  736.5 28.9 %copy-start.8 = (f32[128,1536]{1,0:T(8,128)S(1)}, f32[128,1536]{1,0:T(8,128)}, u32[]{:S(2)}) copy-start(f32[128,1536]{1,0:T(8,128)} %reduce-scatter.8.cloned.1.call-done) | copy-start | bytes 2359300
  765.4 3.1 copy-start.10
  765.4 3.1 copy-start.11
  765.5 4.0 copy-start.9
  765.5 27.4 %copy-start.12 = (f32[128,512]{1,0:T(8,128)S(1)}, f32[128,512]{1,0:T(8,128)}, u32[]{:S(2)}) copy-start(f32[128,512]{1,0:T(8,128)} %get-tuple-element.7) | copy-start | bytes 786436
Sparse Core Ops, SparseCore 0:
  10.5 48.1 all-gather.5
  60.5 45.3 all-gather.7
  108.2 60.3 reduce-scatter.3
  170.4 45.2 all-gather.9
  217.9 60.3 reduce-scatter.5
  281.0 324.5 all-reduce.6
  607.9 59.3 reduce-scatter.7
  673.6 58.6 all-reduce.4
  735.0 27.0 all-gather.11
  765.5 27.3 all-gather.13
